TPU v7x, 32 devices: a whole 2x2x4 slice. The times are simulated.
32 devices in a mesh: dp: 16 (over z, x, core), mp: 2 (over y).
Axes of the slice: x: 2, y: 2, z: 4, core: 2. Of those that a mesh axis runs over, the one named last changes fastest.
Arguments:
- tokens: bfloat16 [2560, 1024], P('dp', 'mp'), may hold values from -6 to 6
- slot_embed: bfloat16 [2560, 1024], P('dp', 'mp'), may hold values from -0.1875 to 0.1875
- price_units: int32 [2560], P('dp'), may hold values from 0 to 1535
- unassigned: int32 [2560], P('dp'), may hold values from 0 to 1, as said below
Outputs:
- new_prices: float32 [2560], P(('dp', 'mp'))
- margins: float32 [2560], P('dp')
- unassigned_count: int32 [], replicated
Inputs may be any that keep to these rules, and one draw needn't show every extreme that they name: At most 128 of the 160 tokens of each index of dp are unassigned, and some index of dp has exactly 128 in every draw.
All inputs are finite; a program needn't handle non-finite values.
Results may differ from a plain program's by a relative error of at most 0.0004.
Values may be sent and summed in bfloat16 or wider, within the bound.
A program may use at most 128 MiB of HBM per device.

v0:
```python
import jax
import jax.numpy as jnp
from jax import lax
from jax.sharding import PartitionSpec as P

BUSY = 128
unit_price = 1.0 / 512.0


def merged(x, axis, combine):
    everything = jax.tree.map(lambda part: lax.all_gather(part, axis), x)
    first = jax.tree.map(lambda part: part[0], everything)

    def turn(k, so_far):
        return combine(so_far, jax.tree.map(lambda part: part[k], everything))

    return lax.fori_loop(1, lax.axis_size(axis), turn, first)


def top_two(values):
    best_value = jnp.max(values, axis=1)
    where_best = jnp.argmax(values, axis=1)
    column_ids = lax.broadcasted_iota(jnp.int32, values.shape, 1)
    second_value = jnp.max(jnp.where(column_ids == where_best[:, None], -jnp.inf, values), axis=1)
    return (best_value, second_value)


def keep_two(first, later):
    best_first, second_first = first
    best_later, second_later = later
    best_value = jnp.maximum(best_first, best_later)
    second_value = jnp.maximum(
        jnp.minimum(best_first, best_later), jnp.maximum(second_first, second_later)
    )
    return (best_value, second_value)


def compact(mask, busy):
    length = mask.shape[0]
    positions = lax.broadcasted_iota(jnp.int32, (length,), 0)
    ordering = jnp.argsort(jnp.where(mask > 0, positions, positions + length))[:busy]
    return (ordering, mask[ordering] > 0)


def spread_back(ordering, is_valid, margin_rows, length):
    positions = lax.broadcasted_iota(jnp.int32, (ordering.shape[0], length), 1)
    hits = (positions == ordering[:, None]) & is_valid[:, None]
    return jnp.sum(jnp.where(hits, margin_rows[:, None], jnp.float32(0.0)), axis=0)


def excess_of(values, second_value, is_valid):
    excess = jnp.where(is_valid[:, None], values - second_value[:, None], -jnp.inf)
    return jnp.max(excess, axis=0)


def on_device(tokens, slot_embed, price_units, unassigned):
    dp_count = lax.axis_size("dp")
    mp_count = lax.axis_size("mp")
    mp_index = lax.axis_index("mp")
    slot_dev = slot_embed.shape[0]
    half = slot_dev // mp_count
    columns = dp_count * half
    ordering, is_valid = compact(unassigned, BUSY)
    bidders = tokens[ordering]
    own_units = lax.dynamic_slice_in_dim(price_units, mp_index * half, half)
    own_prices = own_units.astype(jnp.float32) * unit_price
    whole_bidders = lax.all_gather(bidders, "mp", axis=1, tiled=True)
    slot_rows_whole = lax.all_to_all(slot_embed, "mp", split_axis=0, concat_axis=1, tiled=True)
    unit_all = jnp.zeros((columns,), jnp.int32)
    slot_rows = lax.all_gather(slot_rows_whole, "dp", axis=0, tiled=True)
    unit_rows = lax.all_gather(own_units, "dp", axis=0, tiled=True)
    block = jnp.einsum("bd,sd->bs", whole_bidders, slot_rows, preferred_element_type=jnp.float32)
    unit_all = lax.dynamic_update_slice_in_dim(unit_all, unit_rows, jnp.int32(0), 0)
    scores, unit_all = (block, unit_all)
    values = scores - (unit_all.astype(jnp.float32) * unit_price)[None, :]
    best_value, second_value = merged(top_two(values), "mp", keep_two)
    terms = excess_of(values, second_value, is_valid).reshape(dp_count, half)
    owner_terms = lax.all_to_all(terms, "dp", split_axis=0, concat_axis=0, tiled=True)
    highest = jnp.max(owner_terms, axis=0)
    new_prices = own_prices + jnp.maximum(highest, jnp.float32(0.0))
    margin_rows = jnp.where(is_valid, best_value - second_value, jnp.float32(0.0))
    margins = spread_back(ordering, is_valid, margin_rows, unassigned.shape[0])
    bidder_total = lax.psum(jnp.sum(unassigned), "dp")
    return (new_prices, margins, bidder_total)


def solution(mesh):
    return jax.shard_map(
        on_device,
        mesh=mesh,
        in_specs=(P("dp", "mp"), P("dp", "mp"), P("dp"), P("dp")),
        out_specs=(P(("dp", "mp")), P("dp"), P()),
        check_vma=False,
    )
```

profile of v0, /device:TPU:0, one launch (start us, length us, event | category | flops | bytes accessed | tf_op | source)
XLA Modules:
  0.0 91.2 jit_solution(4303682870376259929)
XLA Ops:
  7.2 0.0 all-gather.7.cloned.1.call-start
  7.2 9.2 %all_to_all.28 = bf16[2,80,512]{2,1,0:T(8,128)(2,1)S(1)} all-to-all(bf16[2,80,512]{2,1,0:T(8,128)(2,1)} %bitcast.19), channel_id=1, replica_groups=mesh['dp'=16,'mp'=2] {'mp'}, dimensions={0} | all-to-all | bytes 327680 | tf_op jit(solution)/shard_map/all_to_all | solution.py:68
  16.4 0.7 copy.12
  17.1 0.0 all-gather.7.cloned.1.call-update
  17.1 1.3 %fusion.6 = (s32[]{:T(128)}, s32[160]{0:T(256)S(1)}) fusion(s32[160]{0:T(256)} %param.7), kind=kLoop, calls=%fused_computation.23 | loop fusion | flops 639 | bytes 1284 | tf_op jit(solution)/shard_map/reduce_sum | solution.py:83
  18.4 3.2 %sort.17 = (s32[160]{0:T(256)}, s32[160]{0:T(256)S(1)}) sort(s32[160]{0:T(256)S(1)} %get-tuple-element.35, s32[160]{0:T(256)S(1)} %iota.27), dimensions={0}, to_apply=%region_0.1 | sort | flops 1280 | bytes 2560 | tf_op jit(solution)/shard_map/jit(argsort)/sort | solution.py:41
  21.6 1.6 %gather_fusion = s32[128]{0:T(128)S(1)} fusion(s32[160]{0:T(256)} %param.7, s32[1024]{0:T(1024)S(1)} %pad_clamp_fusion), kind=kCustom, calls=%fused_computation | custom fusion | bytes 1536 | tf_op jit(solution)/shard_map/gather | solution.py:42
  23.3 0.8 gather_fusion.1
  24.1 1.2 %dynamic-slice = u32[1]{0:T(128)} dynamic-slice(u32[32]{0:T(128)} %constant.16, u32[]{:T(128)S(6)} %add.30), dynamic_slice_sizes={1} | dynamic-slice | bytes 12
  26.0 0.9 dynamic-slice_dynamic-update-slice_fusion
  26.9 13.7 %all-reduce.1 = (s32[1280]{0:T(1024)S(1)}, s32[]{:T(128)}) all-reduce(s32[1280]{0:T(1024)S(1)} %dynamic-slice_dynamic-update-slice_fusion, s32[]{:T(128)} %get-tuple-element.34), channel_id=1, replica_groups=mesh['dp'=16,'mp'=2] {'dp'}, use_global_device_ids=true, to_apply=%add | all-reduce | flops 1281 | bytes 10248
  40.6 5.6 %all-gather = bf16[128,1024]{1,0:T(8,128)(2,1)S(1)} all-gather(bf16[128,512]{1,0:T(8,128)(2,1)S(1)} %gather_fusion.1), channel_id=2, replica_groups=mesh['dp'=16,'mp'=2] {'mp'}, dimensions={1}, use_global_device_ids=true | all-gather | bytes 393216 | tf_op jit(solution)/shard_map/all_gather | solution.py:67
  46.3 14.8 %all-gather.7.cloned.1.call-done = bf16[1280,1024]{1,0:T(8,128)(2,1)} async-done(((bf16[80,1024]{1,0:T(8,128)(2,1)}), bf16[1280,1024]{1,0:T(8,128)(2,1)}) %all-gather.7.cloned.1.call-update) | async-done | bytes 2621456 | tf_op jit(solution)/shard_map/all_gather | solution.py:70
  61.0 2.7 %convolution_subtract_fusion = f32[128,1280]{1,0:T(8,128)S(1)} fusion(bf16[128,1024]{1,0:T(8,128)(2,1)S(1)} %all-gather, bf16[1280,1024]{1,0:T(8,128)(2,1)} %all-gather.7.cloned.1.call-done, f32[1280]{0:T(1024)S(1)} %convert_multiply_fusion), kind=kOutput, calls=%fused_computation.2 | convolution fusion | flops 335708160 | bytes 3544064 | tf_op jit(solution)/shard_map/bd,sd->bs/dot_general | solution.py:72
  63.8 0.4 iota_reduce_fusion
  64.2 4.2 %all-gather.3 = f32[2,1,128]{2,1,0:T(1,128)S(1)} all-gather(f32[1,1,128]{2,1,0:T(1,128)S(1)} %bitcast.21), channel_id=3, replica_groups=mesh['dp'=16,'mp'=2] {'mp'}, dimensions={0}, use_global_device_ids=true | all-gather | bytes 1536 | tf_op jit(solution)/shard_map/all_gather | solution.py:11
  68.4 0.2 select_reduce_fusion.1
  68.6 4.2 %all-gather.4 = f32[2,1,128]{2,1,0:T(1,128)S(1)} all-gather(f32[1,1,128]{2,1,0:T(1,128)S(1)} %bitcast.22), channel_id=4, replica_groups=mesh['dp'=16,'mp'=2] {'mp'}, dimensions={0}, use_global_device_ids=true | all-gather | bytes 1536 | tf_op jit(solution)/shard_map/all_gather | solution.py:11
  72.9 0.1 select_reduce_fusion
  73.0 0.7 all_to_all.24
  73.7 3.6 %all-to-all-start.1 = ((f32[16,1,80]{2,1,0:T(1,128)}), f32[16,1,80]{2,1,0:T(1,128)S(1)}, u32[]{:S(2)}, u32[]{:S(2)}) async-start(f32[16,1,80]{2,1,0:T(1,128)} %all_to_all.24), calls=%async_computation.1 | async-start | bytes 16384 | tf_op jit(solution)/shard_map/all_to_all | solution.py:78
  77.3 0.7 select_reduce_fusion.2
  77.9 5.8 %all-to-all-done.1 = f32[16,1,80]{2,1,0:T(1,128)S(1)} async-done(((f32[16,1,80]{2,1,0:T(1,128)}), f32[16,1,80]{2,1,0:T(1,128)S(1)}, u32[]{:S(2)}, u32[]{:S(2)}) %all-to-all-start.1) | async-done | bytes 5152 | tf_op jit(solution)/shard_map/all_to_all | solution.py:78
  83.7 0.6 maximum_add_fusion
  (12 shorter events, 0.1 us)
Async XLA Ops:
  7.2 16.1 %copy-start = (bf16[160,512]{1,0:T(8,128)(2,1)S(1)}, bf16[160,512]{1,0:T(8,128)(2,1)}, u32[]{:S(2)}) copy-start(bf16[160,512]{1,0:T(8,128)(2,1)} %param.4) | copy-start | bytes 491524
  7.2 53.9 %all-gather.7.cloned.1.call-start = ((), (), s32[]{:S(2)}) async-start(), calls=%async_computation.2 | async-start | bytes 2785280 | tf_op jit(solution)/shard_map/all_gather | solution.py:70
  46.2 37.5 %copy-start.1 = (s32[160]{0:T(256)S(1)}, s32[160]{0:T(256)}, u32[]{:S(2)}) copy-start(s32[160]{0:T(256)} %param.6) | copy-start | bytes 1924
  73.7 10.0 %all-to-all-start.1 = ((f32[16,1,80]{2,1,0:T(1,128)}), f32[16,1,80]{2,1,0:T(1,128)S(1)}, u32[]{:S(2)}, u32[]{:S(2)}) async-start(f32[16,1,80]{2,1,0:T(1,128)} %all_to_all.24), calls=%async_computation.1 | async-start | bytes 16384 | tf_op jit(solution)/shard_map/all_to_all | solution.py:78
Sparse Core Ops, SparseCore 0:
  17.2 43.7 all-gather.6
where the time goes:
time: 91.5 us; the launch traced here: 91.2 us
  blocking collectives  37 us (40%)
  waiting for transfers between devices  20.6 us (23%)
  between operations  14.7 us (16%)
  other arithmetic  6.56 us (7%)
  local copies, waits for them, and re-layouts  5.97 us (7%)
  starting transfers between devices  3.59 us (4%)
  matrix products  2.73 us (3%)
    all_gather x1, waiting for transfers between devices, on_device(): slot_rows = lax.all_gather(slot_rows_whole, 'dp', axis=0, tiled=True)  14.8 us
    unnamed x1, blocking collectives  13.7 us
    all_to_all x1, blocking collectives, on_device(): lax.all_to_all(slot_embed, 'mp', split_axis=0, concat_axis=1, tiled=True)  9.2 us
    all_gather x2, blocking collectives, merged(): everything = jax.tree.map(lambda part: lax.all_gather(part, axis), x)  8.47 us
    all_to_all x1, waiting for transfers between devices, on_device(): lax.all_to_all(terms, 'dp', split_axis=0, concat_axis=0, tiled=True)  5.75 us
    all_gather x1, blocking collectives, on_device(): whole_bidders = lax.all_gather(bidders, 'mp', axis=1, tiled=True)  5.62 us
    all_to_all x1, starting transfers between devices, on_device(): lax.all_to_all(terms, 'dp', split_axis=0, concat_axis=0, tiled=True)  3.55 us
    sort x1, other arithmetic, compact(): jnp.argsort(jnp.where(mask > 0, positions, positions + length))[:busy]  3.17 us
  transfers between devices with their start and end apart: 2, of which 2 were waited for; matrix products, arithmetic and copies ran while one was open for 11% of the time, Pallas kernels for 0%

commit v1 on v0

--- a/solution.py
+++ b/solution.py
@@ -5,6 +5,12 @@
 
 BUSY = 128
 unit_price = 1.0 / 512.0
+
+
+def laid_out(parts, dim):
+    shape = list(parts.shape[1:])
+    shape[dim] *= parts.shape[0]
+    return jnp.moveaxis(parts, 0, dim).reshape(shape)
 
 
 def merged(x, axis, combine):
@@ -67,9 +73,19 @@
     whole_bidders = lax.all_gather(bidders, "mp", axis=1, tiled=True)
     slot_rows_whole = lax.all_to_all(slot_embed, "mp", split_axis=0, concat_axis=1, tiled=True)
     unit_all = jnp.zeros((columns,), jnp.int32)
-    slot_rows = lax.all_gather(slot_rows_whole, "dp", axis=0, tiled=True)
     unit_rows = lax.all_gather(own_units, "dp", axis=0, tiled=True)
-    block = jnp.einsum("bd,sd->bs", whole_bidders, slot_rows, preferred_element_type=jnp.float32)
+    size, here, span = (lax.axis_size("dp"), lax.axis_index("dp"), slot_rows_whole.shape[0])
+    right = [(i, (i + 1) % size) for i in range(size)]
+    blocks = []
+    held = slot_rows_whole
+    for step in range(size):
+        coming = held if step == size - 1 else lax.ppermute(held, "dp", right)
+        blocks.append(
+            jnp.einsum("bd,sd->bs", whole_bidders, held, preferred_element_type=jnp.float32)
+        )
+        held = coming
+    blocks = jnp.stack(blocks)[(here - jnp.arange(size)) % size]
+    block = laid_out(blocks, 1)
     unit_all = lax.dynamic_update_slice_in_dim(unit_all, unit_rows, jnp.int32(0), 0)
     scores, unit_all = (block, unit_all)
     values = scores - (unit_all.astype(jnp.float32) * unit_price)[None, :]

time: 91.5 us -> 168 us (1.84)
  waiting for transfers between devices: 20.6 us -> 114 us
  between operations: 14.7 us -> 1.55 us
  blocking collectives: 37 us -> 28 us
  starting transfers between devices: 3.59 us -> 7.99 us
    ppermute x0 -> x15, waiting for transfers between devices: none -> 108 us  [on_device(): coming = held if step == size - 1 else lax.ppermute(held, 'dp', right)]
    all_gather x1 -> x0, waiting for transfers between devices: 14.8 us -> none  [on_device(): slot_rows = lax.all_gather(slot_rows_whole, 'dp', axis=0, tiled=True)]
    all_to_all x1 -> x0, blocking collectives: 9.2 us -> none  [on_device(): lax.all_to_all(slot_embed, 'mp', split_axis=0, concat_axis=1, tiled=True)]
    all_to_all x0 -> x1, starting transfers between devices: none -> 4.41 us  [on_device(): lax.all_to_all(slot_embed, 'mp', split_axis=0, concat_axis=1, tiled=True)]
    dot_general x1 -> x16, matrix products: 2.73 us -> 3.42 us  [on_device(): jnp.einsum('bd,sd->bs', whole_bidders, held, preferred_element_type=jnp.f...]
  transfers between devices with their start and end apart: 2 -> 17, of which waited for: 2 -> 16; matrix products, arithmetic and copies ran while one was open for 11% -> 6% of each run, Pallas kernels for 0% -> 0%
where the time goes in v1:
time: 168 us
  waiting for transfers between devices  114 us (68%)
  blocking collectives  28 us (17%)
  starting transfers between devices  7.99 us (5%)
  other arithmetic  7.7 us (5%)
  local copies, waits for them, and re-layouts  5.53 us (3%)
  matrix products  3.42 us (2%)
    ppermute x15, waiting for transfers between devices, on_device(): coming = held if step == size - 1 else lax.ppermute(held, 'dp', right)  108 us
    unnamed x1, blocking collectives  13.9 us
    all_gather x2, blocking collectives, merged(): everything = jax.tree.map(lambda part: lax.all_gather(part, axis), x)  8.46 us
    all_to_all x1, waiting for transfers between devices, on_device(): lax.all_to_all(terms, 'dp', split_axis=0, concat_axis=0, tiled=True)  5.72 us
    all_gather x1, blocking collectives, on_device(): whole_bidders = lax.all_gather(bidders, 'mp', axis=1, tiled=True)  5.63 us
    all_to_all x1, starting transfers between devices, on_device(): lax.all_to_all(slot_embed, 'mp', split_axis=0, concat_axis=1, tiled=True)  4.41 us
    all_to_all x1, starting transfers between devices, on_device(): lax.all_to_all(terms, 'dp', split_axis=0, concat_axis=0, tiled=True)  3.49 us
    dot_general x16, matrix products, on_device(): jnp.einsum('bd,sd->bs', whole_bidders, held, preferred_element_type=jnp.f...  3.42 us
  transfers between devices with their start and end apart: 17, of which 16 were waited for; matrix products, arithmetic and copies ran while one was open for 6% of the time, Pallas kernels for 0%

profile of v1, /device:TPU:0, one launch (start us, length us, event | category | flops | bytes accessed | tf_op | source)
XLA Modules:
  0.0 168.1 jit_solution(360631112694692889)
XLA Ops:
  0.6 4.4 %all-to-all-start = ((bf16[2,80,512]{2,1,0:T(8,128)(2,1)}), bf16[2,80,512]{2,1,0:T(8,128)(2,1)S(1)}, u32[]{:S(2)}, u32[]{:S(2)}) async-start(bf16[2,80,512]{2,1,0:T(8,128)(2,1)} %bitcast.129), calls=%async_computation | async-start | bytes 327680 | tf_op jit(solution)/shard_map/all_to_all | solution.py:74
  6.4 3.2 %sort.17 = (s32[160]{0:T(256)}, s32[160]{0:T(256)S(1)}) sort(s32[160]{0:T(256)S(1)} %get-tuple-element.34, s32[160]{0:T(256)S(1)} %iota.46), dimensions={0}, to_apply=%region_0.1 | sort | flops 1280 | bytes 2560 | tf_op jit(solution)/shard_map/jit(argsort)/sort | solution.py:47
  12.3 13.9 %all-reduce.1 = (s32[1280]{0:T(1024)S(1)}, s32[]{:T(128)}) all-reduce(s32[1280]{0:T(1024)S(1)} %dynamic-slice_dynamic-update-slice_fusion, s32[]{:T(128)} %get-tuple-element.33), channel_id=1, replica_groups=mesh['dp'=16,'mp'=2] {'dp'}, use_global_device_ids=true, to_apply=%add | all-reduce | flops 1281 | bytes 10248
  26.2 1.3 gather_fusion
  28.5 5.6 %all-gather = bf16[128,1024]{1,0:T(8,128)(2,1)S(1)} all-gather(bf16[128,512]{1,0:T(8,128)(2,1)S(1)} %gather_fusion.1), channel_id=2, replica_groups=mesh['dp'=16,'mp'=2] {'mp'}, dimensions={1}, use_global_device_ids=true | all-gather | bytes 393216 | tf_op jit(solution)/shard_map/all_gather | solution.py:73
  34.4 7.2 %collective-permute-done = bf16[80,1024]{1,0:T(8,128)(2,1)S(1)} collective-permute-done((bf16[80,1024]{1,0:T(8,128)(2,1)S(1)}, bf16[80,1024]{1,0:T(8,128)(2,1)S(1)}, u32[]{:S(2)}, u32[]{:S(2)}) %collective-permute-start) | collective-permute-done | bytes 163872 | tf_op jit(solution)/shard_map/ppermute | solution.py:82
  41.8 7.2 %collective-permute-done.1 = bf16[80,1024]{1,0:T(8,128)(2,1)S(1)} collective-permute-done((bf16[80,1024]{1,0:T(8,128)(2,1)S(1)}, bf16[80,1024]{1,0:T(8,128)(2,1)S(1)}, u32[]{:S(2)}, u32[]{:S(2)}) %collective-permute-start.1) | collective-permute-done | bytes 163872 | tf_op jit(solution)/shard_map/ppermute | solution.py:82
  49.3 7.2 %collective-permute-done.2 = bf16[80,1024]{1,0:T(8,128)(2,1)S(1)} collective-permute-done((bf16[80,1024]{1,0:T(8,128)(2,1)S(1)}, bf16[80,1024]{1,0:T(8,128)(2,1)S(1)}, u32[]{:S(2)}, u32[]{:S(2)}) %collective-permute-start.2) | collective-permute-done | bytes 163872 | tf_op jit(solution)/shard_map/ppermute | solution.py:82
  56.7 7.2 %collective-permute-done.3 = bf16[80,1024]{1,0:T(8,128)(2,1)S(1)} collective-permute-done((bf16[80,1024]{1,0:T(8,128)(2,1)S(1)}, bf16[80,1024]{1,0:T(8,128)(2,1)S(1)}, u32[]{:S(2)}, u32[]{:S(2)}) %collective-permute-start.3) | collective-permute-done | bytes 163872 | tf_op jit(solution)/shard_map/ppermute | solution.py:82
  64.1 7.2 %collective-permute-done.4 = bf16[80,1024]{1,0:T(8,128)(2,1)S(1)} collective-permute-done((bf16[80,1024]{1,0:T(8,128)(2,1)S(1)}, bf16[80,1024]{1,0:T(8,128)(2,1)S(1)}, u32[]{:S(2)}, u32[]{:S(2)}) %collective-permute-start.4) | collective-permute-done | bytes 163872 | tf_op jit(solution)/shard_map/ppermute | solution.py:82
  71.6 7.2 %collective-permute-done.5 = bf16[80,1024]{1,0:T(8,128)(2,1)S(1)} collective-permute-done((bf16[80,1024]{1,0:T(8,128)(2,1)S(1)}, bf16[80,1024]{1,0:T(8,128)(2,1)S(1)}, u32[]{:S(2)}, u32[]{:S(2)}) %collective-permute-start.5) | collective-permute-done | bytes 163872 | tf_op jit(solution)/shard_map/ppermute | solution.py:82
  79.0 7.2 %collective-permute-done.6 = bf16[80,1024]{1,0:T(8,128)(2,1)S(1)} collective-permute-done((bf16[80,1024]{1,0:T(8,128)(2,1)S(1)}, bf16[80,1024]{1,0:T(8,128)(2,1)S(1)}, u32[]{:S(2)}, u32[]{:S(2)}) %collective-permute-start.6) | collective-permute-done | bytes 163872 | tf_op jit(solution)/shard_map/ppermute | solution.py:82
  86.5 7.2 %collective-permute-done.7 = bf16[80,1024]{1,0:T(8,128)(2,1)S(1)} collective-permute-done((bf16[80,1024]{1,0:T(8,128)(2,1)S(1)}, bf16[80,1024]{1,0:T(8,128)(2,1)S(1)}, u32[]{:S(2)}, u32[]{:S(2)}) %collective-permute-start.7) | collective-permute-done | bytes 163872 | tf_op jit(solution)/shard_map/ppermute | solution.py:82
  93.9 7.2 %collective-permute-done.8 = bf16[80,1024]{1,0:T(8,128)(2,1)S(1)} collective-permute-done((bf16[80,1024]{1,0:T(8,128)(2,1)S(1)}, bf16[80,1024]{1,0:T(8,128)(2,1)S(1)}, u32[]{:S(2)}, u32[]{:S(2)}) %collective-permute-start.8) | collective-permute-done | bytes 163872 | tf_op jit(solution)/shard_map/ppermute | solution.py:82
  101.4 7.2 %collective-permute-done.9 = bf16[80,1024]{1,0:T(8,128)(2,1)S(1)} collective-permute-done((bf16[80,1024]{1,0:T(8,128)(2,1)S(1)}, bf16[80,1024]{1,0:T(8,128)(2,1)S(1)}, u32[]{:S(2)}, u32[]{:S(2)}) %collective-permute-start.9) | collective-permute-done | bytes 163872 | tf_op jit(solution)/shard_map/ppermute | solution.py:82
  108.8 7.2 %collective-permute-done.10 = bf16[80,1024]{1,0:T(8,128)(2,1)S(1)} collective-permute-done((bf16[80,1024]{1,0:T(8,128)(2,1)S(1)}, bf16[80,1024]{1,0:T(8,128)(2,1)S(1)}, u32[]{:S(2)}, u32[]{:S(2)}) %collective-permute-start.10) | collective-permute-done | bytes 163872 | tf_op jit(solution)/shard_map/ppermute | solution.py:82
  116.2 7.2 %collective-permute-done.11 = bf16[80,1024]{1,0:T(8,128)(2,1)S(1)} collective-permute-done((bf16[80,1024]{1,0:T(8,128)(2,1)S(1)}, bf16[80,1024]{1,0:T(8,128)(2,1)S(1)}, u32[]{:S(2)}, u32[]{:S(2)}) %collective-permute-start.11) | collective-permute-done | bytes 163872 | tf_op jit(solution)/shard_map/ppermute | solution.py:82
  123.7 7.2 %collective-permute-done.12 = bf16[80,1024]{1,0:T(8,128)(2,1)S(1)} collective-permute-done((bf16[80,1024]{1,0:T(8,128)(2,1)S(1)}, bf16[80,1024]{1,0:T(8,128)(2,1)S(1)}, u32[]{:S(2)}, u32[]{:S(2)}) %collective-permute-start.12) | collective-permute-done | bytes 163872 | tf_op jit(solution)/shard_map/ppermute | solution.py:82
  131.1 7.2 %collective-permute-done.13 = bf16[80,1024]{1,0:T(8,128)(2,1)S(1)} collective-permute-done((bf16[80,1024]{1,0:T(8,128)(2,1)S(1)}, bf16[80,1024]{1,0:T(8,128)(2,1)S(1)}, u32[]{:S(2)}, u32[]{:S(2)}) %collective-permute-start.13) | collective-permute-done | bytes 163872 | tf_op jit(solution)/shard_map/ppermute | solution.py:82
  138.6 7.2 %collective-permute-done.14 = bf16[80,1024]{1,0:T(8,128)(2,1)S(1)} collective-permute-done((bf16[80,1024]{1,0:T(8,128)(2,1)S(1)}, bf16[80,1024]{1,0:T(8,128)(2,1)S(1)}, u32[]{:S(2)}, u32[]{:S(2)}) %collective-permute-start.14) | collective-permute-done | bytes 163872 | tf_op jit(solution)/shard_map/ppermute | solution.py:82
  148.0 4.2 %all-gather.3 = f32[2,1,128]{2,1,0:T(1,128)S(1)} all-gather(f32[1,1,128]{2,1,0:T(1,128)S(1)} %bitcast.131), channel_id=3, replica_groups=mesh['dp'=16,'mp'=2] {'mp'}, dimensions={0}, use_global_device_ids=true | all-gather | bytes 1536 | tf_op jit(solution)/shard_map/all_gather | solution.py:17
  152.2 4.2 %all-gather.4 = f32[2,1,128]{2,1,0:T(1,128)S(1)} all-gather(f32[1,1,128]{2,1,0:T(1,128)S(1)} %bitcast.130), channel_id=4, replica_groups=mesh['dp'=16,'mp'=2] {'mp'}, dimensions={0}, use_global_device_ids=true | all-gather | bytes 1536 | tf_op jit(solution)/shard_map/all_gather | solution.py:17
  157.6 3.5 %all-to-all-start.1 = ((f32[16,1,80]{2,1,0:T(1,128)}), f32[16,1,80]{2,1,0:T(1,128)S(1)}, u32[]{:S(2)}, u32[]{:S(2)}) async-start(f32[16,1,80]{2,1,0:T(1,128)} %bitcast.25), calls=%async_computation.1 | async-start | bytes 16384 | tf_op jit(solution)/shard_map/all_to_all | solution.py:94
  161.8 5.7 %all-to-all-done.1 = f32[16,1,80]{2,1,0:T(1,128)S(1)} async-done(((f32[16,1,80]{2,1,0:T(1,128)}), f32[16,1,80]{2,1,0:T(1,128)S(1)}, u32[]{:S(2)}, u32[]{:S(2)}) %all-to-all-start.1) | async-done | bytes 5152 | tf_op jit(solution)/shard_map/all_to_all | solution.py:94
  (63 shorter events, 12.3 us)
Async XLA Ops:
  0.6 26.9 %copy-start = (bf16[160,512]{1,0:T(8,128)(2,1)S(1)}, bf16[160,512]{1,0:T(8,128)(2,1)}, u32[]{:S(2)}) copy-start(bf16[160,512]{1,0:T(8,128)(2,1)} %param.4) | copy-start | bytes 491524
  0.6 33.4 %all-to-all-start = ((bf16[2,80,512]{2,1,0:T(8,128)(2,1)}), bf16[2,80,512]{2,1,0:T(8,128)(2,1)S(1)}, u32[]{:S(2)}, u32[]{:S(2)}) async-start(bf16[2,80,512]{2,1,0:T(8,128)(2,1)} %bitcast.129), calls=%async_computation | async-start | bytes 327680 | tf_op jit(solution)/shard_map/all_to_all | solution.py:74
  5.1 0.7 copy-start.1
  9.6 0.7 copy-start.3
  11.5 0.7 copy-start.2
  34.1 7.5 %collective-permute-start = (bf16[80,1024]{1,0:T(8,128)(2,1)S(1)}, bf16[80,1024]{1,0:T(8,128)(2,1)S(1)}, u32[]{:S(2)}, u32[]{:S(2)}) collective-permute-start(bf16[80,1024]{1,0:T(8,128)(2,1)S(1)} %bitcast.126), channel_id=1, source_target_pairs={{0,2},{2,4},{4,6},{6,8},{8,10},{10,12},{12,14},{14,16},{16,18},{18... | collective-permute-start | bytes 491528 | tf_op jit(solution)/shard_map/ppermute | solution.py:82
  41.6 7.4 %collective-permute-start.1 = (bf16[80,1024]{1,0:T(8,128)(2,1)S(1)}, bf16[80,1024]{1,0:T(8,128)(2,1)S(1)}, u32[]{:S(2)}, u32[]{:S(2)}) collective-permute-start(bf16[80,1024]{1,0:T(8,128)(2,1)S(1)} %collective-permute-done), channel_id=1, source_target_pairs={{0,2},{2,4},{4,6},{6,8},{8,10},{10,12},{12,14},{14,16},{16,18},{18... | collective-permute-start | bytes 491528 | tf_op jit(solution)/shard_map/ppermute | solution.py:82
  49.0 7.4 %collective-permute-start.2 = (bf16[80,1024]{1,0:T(8,128)(2,1)S(1)}, bf16[80,1024]{1,0:T(8,128)(2,1)S(1)}, u32[]{:S(2)}, u32[]{:S(2)}) collective-permute-start(bf16[80,1024]{1,0:T(8,128)(2,1)S(1)} %collective-permute-done.1), channel_id=1, source_target_pairs={{0,2},{2,4},{4,6},{6,8},{8,10},{10,12},{12,14},{14,16},{16,18},{18... | collective-permute-start | bytes 491528 | tf_op jit(solution)/shard_map/ppermute | solution.py:82
  56.5 7.4 %collective-permute-start.3 = (bf16[80,1024]{1,0:T(8,128)(2,1)S(1)}, bf16[80,1024]{1,0:T(8,128)(2,1)S(1)}, u32[]{:S(2)}, u32[]{:S(2)}) collective-permute-start(bf16[80,1024]{1,0:T(8,128)(2,1)S(1)} %collective-permute-done.2), channel_id=1, source_target_pairs={{0,2},{2,4},{4,6},{6,8},{8,10},{10,12},{12,14},{14,16},{16,18},{18... | collective-permute-start | bytes 491528 | tf_op jit(solution)/shard_map/ppermute | solution.py:82
  63.9 7.4 %collective-permute-start.4 = (bf16[80,1024]{1,0:T(8,128)(2,1)S(1)}, bf16[80,1024]{1,0:T(8,128)(2,1)S(1)}, u32[]{:S(2)}, u32[]{:S(2)}) collective-permute-start(bf16[80,1024]{1,0:T(8,128)(2,1)S(1)} %collective-permute-done.3), channel_id=1, source_target_pairs={{0,2},{2,4},{4,6},{6,8},{8,10},{10,12},{12,14},{14,16},{16,18},{18... | collective-permute-start | bytes 491528 | tf_op jit(solution)/shard_map/ppermute | solution.py:82
  71.4 7.4 %collective-permute-start.5 = (bf16[80,1024]{1,0:T(8,128)(2,1)S(1)}, bf16[80,1024]{1,0:T(8,128)(2,1)S(1)}, u32[]{:S(2)}, u32[]{:S(2)}) collective-permute-start(bf16[80,1024]{1,0:T(8,128)(2,1)S(1)} %collective-permute-done.4), channel_id=1, source_target_pairs={{0,2},{2,4},{4,6},{6,8},{8,10},{10,12},{12,14},{14,16},{16,18},{18... | collective-permute-start | bytes 491528 | tf_op jit(solution)/shard_map/ppermute | solution.py:82
  78.8 7.4 %collective-permute-start.6 = (bf16[80,1024]{1,0:T(8,128)(2,1)S(1)}, bf16[80,1024]{1,0:T(8,128)(2,1)S(1)}, u32[]{:S(2)}, u32[]{:S(2)}) collective-permute-start(bf16[80,1024]{1,0:T(8,128)(2,1)S(1)} %collective-permute-done.5), channel_id=1, source_target_pairs={{0,2},{2,4},{4,6},{6,8},{8,10},{10,12},{12,14},{14,16},{16,18},{18... | collective-permute-start | bytes 491528 | tf_op jit(solution)/shard_map/ppermute | solution.py:82
  86.2 7.4 %collective-permute-start.7 = (bf16[80,1024]{1,0:T(8,128)(2,1)S(1)}, bf16[80,1024]{1,0:T(8,128)(2,1)S(1)}, u32[]{:S(2)}, u32[]{:S(2)}) collective-permute-start(bf16[80,1024]{1,0:T(8,128)(2,1)S(1)} %collective-permute-done.6), channel_id=1, source_target_pairs={{0,2},{2,4},{4,6},{6,8},{8,10},{10,12},{12,14},{14,16},{16,18},{18... | collective-permute-start | bytes 491528 | tf_op jit(solution)/shard_map/ppermute | solution.py:82
  93.7 7.4 %collective-permute-start.8 = (bf16[80,1024]{1,0:T(8,128)(2,1)S(1)}, bf16[80,1024]{1,0:T(8,128)(2,1)S(1)}, u32[]{:S(2)}, u32[]{:S(2)}) collective-permute-start(bf16[80,1024]{1,0:T(8,128)(2,1)S(1)} %collective-permute-done.7), channel_id=1, source_target_pairs={{0,2},{2,4},{4,6},{6,8},{8,10},{10,12},{12,14},{14,16},{16,18},{18... | collective-permute-start | bytes 491528 | tf_op jit(solution)/shard_map/ppermute | solution.py:82
  101.1 7.4 %collective-permute-start.9 = (bf16[80,1024]{1,0:T(8,128)(2,1)S(1)}, bf16[80,1024]{1,0:T(8,128)(2,1)S(1)}, u32[]{:S(2)}, u32[]{:S(2)}) collective-permute-start(bf16[80,1024]{1,0:T(8,128)(2,1)S(1)} %collective-permute-done.8), channel_id=1, source_target_pairs={{0,2},{2,4},{4,6},{6,8},{8,10},{10,12},{12,14},{14,16},{16,18},{18... | collective-permute-start | bytes 491528 | tf_op jit(solution)/shard_map/ppermute | solution.py:82
  108.6 7.4 %collective-permute-start.10 = (bf16[80,1024]{1,0:T(8,128)(2,1)S(1)}, bf16[80,1024]{1,0:T(8,128)(2,1)S(1)}, u32[]{:S(2)}, u32[]{:S(2)}) collective-permute-start(bf16[80,1024]{1,0:T(8,128)(2,1)S(1)} %collective-permute-done.9), channel_id=1, source_target_pairs={{0,2},{2,4},{4,6},{6,8},{8,10},{10,12},{12,14},{14,16},{16,18},{18... | collective-permute-start | bytes 491528 | tf_op jit(solution)/shard_map/ppermute | solution.py:82
  116.0 7.4 %collective-permute-start.11 = (bf16[80,1024]{1,0:T(8,128)(2,1)S(1)}, bf16[80,1024]{1,0:T(8,128)(2,1)S(1)}, u32[]{:S(2)}, u32[]{:S(2)}) collective-permute-start(bf16[80,1024]{1,0:T(8,128)(2,1)S(1)} %collective-permute-done.10), channel_id=1, source_target_pairs={{0,2},{2,4},{4,6},{6,8},{8,10},{10,12},{12,14},{14,16},{16,18},{18... | collective-permute-start | bytes 491528 | tf_op jit(solution)/shard_map/ppermute | solution.py:82
  123.5 7.4 %collective-permute-start.12 = (bf16[80,1024]{1,0:T(8,128)(2,1)S(1)}, bf16[80,1024]{1,0:T(8,128)(2,1)S(1)}, u32[]{:S(2)}, u32[]{:S(2)}) collective-permute-start(bf16[80,1024]{1,0:T(8,128)(2,1)S(1)} %collective-permute-done.11), channel_id=1, source_target_pairs={{0,2},{2,4},{4,6},{6,8},{8,10},{10,12},{12,14},{14,16},{16,18},{18... | collective-permute-start | bytes 491528 | tf_op jit(solution)/shard_map/ppermute | solution.py:82
  130.9 7.4 %collective-permute-start.13 = (bf16[80,1024]{1,0:T(8,128)(2,1)S(1)}, bf16[80,1024]{1,0:T(8,128)(2,1)S(1)}, u32[]{:S(2)}, u32[]{:S(2)}) collective-permute-start(bf16[80,1024]{1,0:T(8,128)(2,1)S(1)} %collective-permute-done.12), channel_id=1, source_target_pairs={{0,2},{2,4},{4,6},{6,8},{8,10},{10,12},{12,14},{14,16},{16,18},{18... | collective-permute-start | bytes 491528 | tf_op jit(solution)/shard_map/ppermute | solution.py:82
  138.3 7.4 %collective-permute-start.14 = (bf16[80,1024]{1,0:T(8,128)(2,1)S(1)}, bf16[80,1024]{1,0:T(8,128)(2,1)S(1)}, u32[]{:S(2)}, u32[]{:S(2)}) collective-permute-start(bf16[80,1024]{1,0:T(8,128)(2,1)S(1)} %collective-permute-done.13), channel_id=1, source_target_pairs={{0,2},{2,4},{4,6},{6,8},{8,10},{10,12},{12,14},{14,16},{16,18},{18... | collective-permute-start | bytes 491528 | tf_op jit(solution)/shard_map/ppermute | solution.py:82
  157.6 9.9 %all-to-all-start.1 = ((f32[16,1,80]{2,1,0:T(1,128)}), f32[16,1,80]{2,1,0:T(1,128)S(1)}, u32[]{:S(2)}, u32[]{:S(2)}) async-start(f32[16,1,80]{2,1,0:T(1,128)} %bitcast.25), calls=%async_computation.1 | async-start | bytes 16384 | tf_op jit(solution)/shard_map/all_to_all | solution.py:94
